TPU v7x, 128 devices: a whole 4x4x4 slice. The times are simulated.
128 devices in a mesh: blk: 32 (over x, z, core), grp: 4 (over y).
Axes of the slice: x: 4, y: 4, z: 4, core: 2. Of those that a mesh axis runs over, the one named last changes fastest.
Arguments:
- statistics: float32 [4, 64, 512, 512], P('grp', 'blk'), as said below
- gradients: bfloat16 [4, 16, 512, 14336], P('grp', None, None, 'blk'), may hold values from -6 to 6
- live_counts: int32 [4, 32], P('grp'), may hold values from 0 to 2, as said below
- slot_row: int32 [4, 64], P('grp'), may hold values from 0 to 15, as said below
- sweeps: int32 [4, 64], P('grp', 'blk'), may hold values from 1 to 2, as said below
Outputs:
- updates: bfloat16 [4, 16, 512, 14336], P('grp', None, None, 'blk')
- off_max: float32 [2], replicated
Inputs may be any that keep to these rules, and one draw needn't show every extreme that they name: `live_counts`: the live slots of one index of grp number exactly 16; in every draw some device of each grp index has 2 live slots. `slot_row`: over the live slots of one index of grp each row block 0 to 15 appears exactly once. In each index of grp some live slot has 2 sweeps. `statistics`: every block is symmetric positive definite.
All inputs are finite; a program needn't handle non-finite values.
Results may differ from a plain program's by a relative error of at most 0.0051.
Values may be sent and summed in bfloat16 or wider, within the bound.
A program may use at most 192 MiB of HBM per device.

v0:
```python
import functools
import jax
import jax.numpy as jnp
from jax import lax
from jax.sharding import Mesh
from jax.sharding import PartitionSpec as P

MAXS = 2
BLK = ("blk_0", "blk_1", "blk_2")
BLK_GRP = ("blk_0", "blk_1", "blk_2", "grp")
damping = 0.01
pairings = ((0, 1, 2, 3), (0, 2, 1, 3), (0, 3, 1, 2))
highest = lax.Precision.HIGHEST


def by_axis(x, axes):
    return functools.reduce(lax.pmax, axes, x)


def regroup_cols(values, pairing, group_width):
    return jnp.concatenate(
        [values[:, member * group_width : (member + 1) * group_width] for member in pairing], axis=1
    )


def regroup(values, pairing, group_width):
    stacked = jnp.concatenate(
        [values[member * group_width : (member + 1) * group_width] for member in pairing], axis=0
    )
    return regroup_cols(stacked, pairing, group_width)


def angle_block(square_sub):
    group_width = square_sub.shape[-1] // 2
    diagonal = jnp.diagonal(square_sub, axis1=1, axis2=2)
    lower_diag = diagonal[:, :group_width, None]
    upper_diag = diagonal[:, None, group_width:]
    coupling = square_sub[:, :group_width, group_width:]
    difference = upper_diag - lower_diag
    bottom = (
        difference * difference
        + 4.0 * coupling * coupling
        + damping * (lower_diag + upper_diag) ** 2
    )
    return coupling * difference / bottom


def rotation_of(square_sub):
    angles = angle_block(square_sub)
    group_width = angles.shape[-1]
    identity = jnp.eye(group_width, dtype=jnp.float32)
    outer = jnp.einsum("hpq,hrq->hpr", angles, angles, precision=highest)
    inner = jnp.einsum("hqp,hqr->hpr", angles, angles, precision=highest)
    left_factor = jnp.linalg.cholesky(identity + 0.25 * outer)
    right_factor = jnp.linalg.cholesky(identity + 0.25 * inner)
    top_rows = jnp.concatenate([identity - 0.25 * outer, angles], axis=2)
    low_rows = jnp.concatenate([-jnp.swapaxes(angles, 1, 2), identity - 0.25 * inner], axis=2)
    top_half = jax.scipy.linalg.cho_solve((left_factor, True), top_rows)
    low_half = jax.scipy.linalg.cho_solve((right_factor, True), low_rows)
    return jnp.concatenate([top_half, low_half], axis=1)


def rotate_round(matrix, vectors, pairing):
    block_size = matrix.shape[0]
    group_width = block_size // 4
    restore = [pairing.index(member) for member in range(4)]
    matrix = regroup(matrix, pairing, group_width)
    vectors = regroup_cols(vectors, pairing, group_width)
    half_size = 2 * group_width
    square_sub = jnp.stack([matrix[:half_size, :half_size], matrix[half_size:, half_size:]])
    rotation = rotation_of(square_sub)
    row_part = jnp.einsum(
        "hpq,hpc->hqc", rotation, matrix.reshape(2, half_size, block_size), precision=highest
    )
    row_part = row_part.reshape(block_size, block_size)
    matrix = jnp.einsum(
        "rhp,hpq->rhq", row_part.reshape(block_size, 2, half_size), rotation, precision=highest
    )
    matrix = matrix.reshape(block_size, block_size)
    vectors = jnp.einsum(
        "rhp,hpq->rhq", vectors.reshape(block_size, 2, half_size), rotation, precision=highest
    )
    vectors = vectors.reshape(block_size, block_size)
    return (regroup(matrix, restore, group_width), regroup_cols(vectors, restore, group_width))


def one_sweep(matrix, vectors):
    for pairing in pairings:
        matrix, vectors = rotate_round(matrix, vectors, pairing)
    return (matrix, vectors)


def keep_both(matrix, vectors):
    return (matrix, vectors)


def off_norm(matrix):
    block_size = matrix.shape[0]
    on_diagonal = lax.broadcasted_iota(
        jnp.int32, (block_size, block_size), 0
    ) == lax.broadcasted_iota(jnp.int32, (block_size, block_size), 1)
    outside = jnp.where(on_diagonal, 0.0, matrix)
    return jnp.sqrt(jnp.sum(outside * outside) / jnp.sum(matrix * matrix))


def root_factor(matrix, vectors):
    scales = jnp.power(jnp.diagonal(matrix), -0.25)
    return jnp.dot(vectors * scales[None, :], vectors.T, precision=highest).astype(jnp.bfloat16)


def per_device(statistics, gradients, live_counts, slot_row, sweeps):
    matrices = statistics[0]
    slot_count = matrices.shape[0]
    block_size = matrices.shape[1]
    row_count = gradients.shape[1]
    blk_rank = lax.axis_index(BLK)
    own_live = lax.dynamic_index_in_dim(live_counts[0], blk_rank, 0, keepdims=False)
    own_sweeps = sweeps[0]
    identity = jnp.eye(block_size, dtype=jnp.float32)
    states = [matrices[slot_index] for slot_index in range(slot_count)]
    eigen_bases = [identity for slot_index in range(slot_count)]
    live_flags = [slot_index < own_live for slot_index in range(slot_count)]
    sweep_list = [own_sweeps[slot_index] for slot_index in range(slot_count)]
    local_peaks = jnp.zeros((MAXS,), jnp.float32)
    for slot_index in range(slot_count):
        for sweep_index in range(MAXS):
            active = jnp.logical_and(live_flags[slot_index], sweep_list[slot_index] > sweep_index)
            states[slot_index], eigen_bases[slot_index] = lax.cond(
                active, one_sweep, keep_both, states[slot_index], eigen_bases[slot_index]
            )
            local_peaks = local_peaks.at[sweep_index].max(
                jnp.where(active, off_norm(states[slot_index]), jnp.float32(0.0))
            )
    off_max = by_axis(local_peaks, BLK_GRP)
    blank_factor = jnp.zeros((block_size, block_size), jnp.bfloat16)
    factor_list = [
        jnp.where(
            live_flags[slot_index],
            root_factor(states[slot_index], eigen_bases[slot_index]),
            blank_factor,
        )
        for slot_index in range(slot_count)
    ]
    factors = jnp.stack(factor_list)
    row_ids = lax.iota(jnp.int32, row_count)
    gathered = lax.all_gather(factors, BLK, axis=0, tiled=True)
    slot_total = gathered.shape[0]
    slot_ids = lax.iota(jnp.int32, slot_total)
    is_live = slot_ids % slot_count < jnp.repeat(live_counts[0], slot_count)
    matches = (slot_row[0][None, :] == row_ids[:, None]) & is_live[None, :]
    slot_of = jnp.sum(jnp.where(matches, slot_ids[None, :], 0), axis=1)
    chosen = jnp.take(gathered, slot_of, axis=0)
    updates = jnp.einsum("kij,kjc->kic", chosen, gradients[0], preferred_element_type=jnp.float32)
    return (updates.astype(jnp.bfloat16)[None], off_max)


def solution(mesh):
    split = Mesh(
        mesh.devices.reshape(4, 4, 2, mesh.shape["grp"]), ("blk_0", "blk_1", "blk_2", "grp")
    )
    return jax.shard_map(
        per_device,
        mesh=split,
        in_specs=(
            P("grp", BLK, None, None),
            P("grp", None, None, BLK),
            P("grp", None),
            P("grp", None),
            P("grp", BLK),
        ),
        out_specs=(P("grp", None, None, BLK), P()),
        check_vma=False,
    )
```

profile of v0, /device:TPU:1, one launch (start us, length us, event | category | flops | bytes accessed | tf_op | source)
XLA Modules:
  0.0 1782.7 jit_solution(11419021902682509797)
XLA Ops:
  14.5 2.7 slice_bitcast_fusion.9
  17.2 372.8 %conditional.4 = (f32[512,512]{0,1:T(8,128)S(1)}, f32[512,512]{0,1:T(8,128)S(1)}) conditional(s32[]{:T(128)} %convert_element_type.155, (f32[512,512]{1,0:T(8,128)S(1)}, f32[512,512]{0,1:T(8,128)S(1)}) %tuple.70, (f32[512,512]{1,0:T(8,128)S(1)}, f32[512,512]{0,1:T(8,128)S(1)}) %tuple.70), branch_computations={%region_1.2_spmd, %region_2.7_spmd} | conditional | flops 8781105152 | bytes 108000352 | solution.py:128
  18.2 17.2 copy.767
  38.6 23.5 %custom-call.84 = f32[2,128,128]{2,1,0:T(8,128)S(1)} custom-call(f32[2,128,128]{2,1,0:T(8,128)S(1)} %fusion.75), custom_call_target="Cholesky" | custom-call | tf_op jit(solution)/shard_map/cond/branch_1_fun/jit(cholesky)/cholesky | solution.py:55
  62.6 23.5 %custom-call.82 = f32[2,128,128]{2,1,0:T(8,128)S(1)} custom-call(f32[2,128,128]{2,1,0:T(8,128)S(1)} %copy.773), custom_call_target="Cholesky" | custom-call | tf_op jit(solution)/shard_map/cond/branch_1_fun/jit(cholesky)/cholesky | solution.py:54
  87.0 20.1 %custom-call.83 = f32[2,1,128,128]{2,3,1,0:T(8,128)S(1)} custom-call(f32[2,1,128,128]{3,2,1,0:T(8,128)S(1)} %get-tuple-element.295), custom_call_target="InvertDiagBlocksLowerTriangular" | custom-call | tf_op jit(solution)/shard_map/cond/branch_1_fun/jit(_cho_solve)/vmap()/triangular_solve | solution.py:58
  108.0 20.5 %custom-call.85 = f32[2,1,128,128]{2,3,1,0:T(8,128)S(1)} custom-call(f32[2,1,128,128]{3,2,1,0:T(8,128)} %get-tuple-element.296), custom_call_target="InvertDiagBlocksLowerTriangular" | custom-call | tf_op jit(solution)/shard_map/cond/branch_1_fun/jit(_cho_solve)/vmap()/triangular_solve | solution.py:59
  142.2 16.6 copy.788
  163.4 23.5 %custom-call.86 = f32[2,128,128]{2,1,0:T(8,128)S(1)} custom-call(f32[2,128,128]{2,1,0:T(8,128)S(1)} %fusion.71), custom_call_target="Cholesky" | custom-call | tf_op jit(solution)/shard_map/cond/branch_1_fun/jit(cholesky)/cholesky | solution.py:54
  187.0 23.5 %custom-call.88 = f32[2,128,128]{2,1,0:T(8,128)S(1)} custom-call(f32[2,128,128]{2,1,0:T(8,128)S(1)} %fusion.67), custom_call_target="Cholesky" | custom-call | tf_op jit(solution)/shard_map/cond/branch_1_fun/jit(cholesky)/cholesky | solution.py:55
  210.9 19.9 %custom-call.87 = f32[2,1,128,128]{2,3,1,0:T(8,128)S(1)} custom-call(f32[2,1,128,128]{3,2,1,0:T(8,128)S(1)} %get-tuple-element.293), custom_call_target="InvertDiagBlocksLowerTriangular" | custom-call | tf_op jit(solution)/shard_map/cond/branch_1_fun/jit(_cho_solve)/vmap()/triangular_solve | solution.py:58
  231.6 19.7 %custom-call.89 = f32[2,1,128,128]{2,3,1,0:T(8,128)S(1)} custom-call(f32[2,1,128,128]{3,2,1,0:T(8,128)S(1)} %get-tuple-element.294), custom_call_target="InvertDiagBlocksLowerTriangular" | custom-call | tf_op jit(solution)/shard_map/cond/branch_1_fun/jit(_cho_solve)/vmap()/triangular_solve | solution.py:59
  255.1 3.4 fusion.14
  267.4 16.5 copy.812
  287.0 23.9 %custom-call.92 = f32[2,128,128]{2,1,0:T(8,128)S(1)} custom-call(f32[2,128,128]{2,1,0:T(8,128)S(1)} %fusion.59), custom_call_target="Cholesky" | custom-call | tf_op jit(solution)/shard_map/cond/branch_1_fun/jit(cholesky)/cholesky | solution.py:55
  311.5 23.5 %custom-call.90 = f32[2,128,128]{2,1,0:T(8,128)S(1)} custom-call(f32[2,128,128]{2,1,0:T(8,128)S(1)} %copy.818), custom_call_target="Cholesky" | custom-call | tf_op jit(solution)/shard_map/cond/branch_1_fun/jit(cholesky)/cholesky | solution.py:54
  336.8 19.7 %custom-call.91 = f32[2,1,128,128]{2,3,1,0:T(8,128)S(1)} custom-call(f32[2,1,128,128]{3,2,1,0:T(8,128)S(1)} %get-tuple-element.291), custom_call_target="InvertDiagBlocksLowerTriangular" | custom-call | tf_op jit(solution)/shard_map/cond/branch_1_fun/jit(_cho_solve)/vmap()/triangular_solve | solution.py:58
  357.3 19.8 %custom-call.93 = f32[2,1,128,128]{2,3,1,0:T(8,128)S(1)} custom-call(f32[2,1,128,128]{3,2,1,0:T(8,128)S(1)} %get-tuple-element.292), custom_call_target="InvertDiagBlocksLowerTriangular" | custom-call | tf_op jit(solution)/shard_map/cond/branch_1_fun/jit(_cho_solve)/vmap()/triangular_solve | solution.py:59
  380.1 3.4 fusion.12
  392.6 15.4 conditional.5
  408.0 8.9 gather_fusion.12
  416.9 10.5 conditional.6
  431.3 11.1 conditional.7
  442.4 8.5 gather_fusion.13
  452.9 2.6 fusion.410
  470.0 811.0 %pmax.28 = f32[2]{0:T(128)S(1)} all-reduce(f32[2]{0:T(128)S(1)} %maximum_dynamic-update-slice_fusion), channel_id=1, replica_groups=mesh['blk_0'=4,'blk_1'=4,'blk_2'=2,'grp'=4] {'blk_0'}, use_global_device_ids=true, to_apply=%region_19.22 | all-reduce | flops 2 | bytes 16 | tf_op jit(solution)/shard_map/pmax | solution.py:17
  1281.0 6.0 pmax.29
  1286.9 9.1 pmax.30
  1296.0 390.1 %pmax.31 = f32[2]{0:T(128)} all-reduce(f32[2]{0:T(128)S(1)} %pmax.30), channel_id=1, replica_groups=mesh['blk_0'=4,'blk_1'=4,'blk_2'=2,'grp'=4] {'grp'}, use_global_device_ids=true, to_apply=%region_22.25 | all-reduce | flops 2 | bytes 16 | tf_op jit(solution)/shard_map/pmax | solution.py:17
  1687.2 71.6 %all-gather.2.cloned.1.call-done = bf16[64,512,512]{2,1,0:T(8,128)(2,1)} async-done(((bf16[2,512,512]{2,1,0:T(8,128)(2,1)}), bf16[64,512,512]{2,1,0:T(8,128)(2,1)}) %all-gather.2.cloned.1.call-update) | async-done | bytes 33554448 | tf_op jit(solution)/shard_map/all_gather | solution.py:146
  1758.8 6.3 gather_fusion.14
  1765.0 10.6 convert_bitcast_fusion
  (153 shorter events, 80.9 us)
Async XLA Ops:
  7.2 1751.6 %all-gather.2.cloned.1.call-start = ((), (), s32[]{:S(2)}) async-start(), calls=%async_computation | async-start | bytes 34603008 | tf_op jit(solution)/shard_map/all_gather | solution.py:146
  17.2 193.3 %copy-start.17 = (pred[128,128]{1,0:T(8,128)(4,1)}, pred[128,128]{1,0:T(8,128)(4,1)S(1)}, u32[]{:S(2)}) copy-start(pred[128,128]{1,0:T(8,128)(4,1)S(1)} %iota_compare_fusion.7) | copy-start | bytes 49156 | tf_op jit(solution)/shard_map/cond
  17.2 193.5 %copy-start.13 = (pred[128,128]{1,0:T(8,128)(4,1)}, pred[128,128]{1,0:T(8,128)(4,1)S(1)}, u32[]{:S(2)}) copy-start(pred[128,128]{1,0:T(8,128)(4,1)S(1)} %iota_compare_fusion.6) | copy-start | bytes 49156 | tf_op jit(solution)/shard_map/cond
  431.3 1254.9 %copy-start.21 = (s32[1,32]{1,0:T(1,128)S(1)}, s32[1,32]{1,0:T(1,128)}, u32[]{:S(2)}) copy-start(s32[1,32]{1,0:T(1,128)} %param.26) | copy-start | bytes 388
Sparse Core Ops, SparseCore 0:
  456.7 1302.0 all-gather.1
where the time goes:
time: 1800 us; the launch traced here: 1780 us
  blocking collectives  1220 us (68%)
  other arithmetic  282 us (16%)
  local copies, waits for them, and re-layouts  112 us (6%)
  waiting for transfers between devices  71.6 us (4%)
  matrix products  44.1 us (2%)
  loops' own time  32.1 us (2%)
  between operations  24.6 us (1%)
    pmax x4, blocking collectives, by_axis(): return functools.reduce(lax.pmax, axes, x)  1220 us
    all_gather x1, waiting for transfers between devices, per_device(): gathered = lax.all_gather(factors, BLK, axis=0, tiled=True)  71.6 us
    another operation x9, other arithmetic, rotation_of(): left_factor = jnp.linalg.cholesky(identity + 0.25 * outer)  71.5 us
    another operation x6, other arithmetic, rotation_of(): right_factor = jnp.linalg.cholesky(identity + 0.25 * inner)  71.2 us
    another operation x7, other arithmetic, rotation_of(): top_half = jax.scipy.linalg.cho_solve((left_factor, True), top_rows)  61.4 us
    another operation x3, other arithmetic, rotation_of(): low_half = jax.scipy.linalg.cho_solve((right_factor, True), low_rows)  60 us
    another operation x4, local copies, waits for them, and re-layouts, rotate_round(): jnp.stack([matrix[:half_size, :half_size], matrix[half_size:, half_size:]])  50.3 us
  transfers between devices with their start and end apart: 1, of which 1 were waited for; matrix products, arithmetic and copies ran while one was open for 0% of the time, Pallas kernels for 0%

commit v1 on v0

--- a/solution.py
+++ b/solution.py
@@ -143,7 +143,9 @@
     ]
     factors = jnp.stack(factor_list)
     row_ids = lax.iota(jnp.int32, row_count)
-    gathered = lax.all_gather(factors, BLK, axis=0, tiled=True)
+    gathered = jnp.concatenate(
+        lax.all_to_all(jnp.stack([factors] * lax.axis_size(BLK)), BLK, 0, 0), axis=0
+    )
     slot_total = gathered.shape[0]
     slot_ids = lax.iota(jnp.int32, slot_total)
     is_live = slot_ids % slot_count < jnp.repeat(live_counts[0], slot_count)

time: 1800 us -> 2320 us (1.29)
  starting transfers between devices: 0.04 us -> 840 us
  blocking collectives: 1220 us -> 950 us
  waiting for transfers between devices: 71.6 us -> 0.01 us
    all_to_all x0 -> x1, starting transfers between devices: none -> 840 us  [per_device(): lax.all_to_all(jnp.stack([factors] * lax.axis_size(BLK)), BLK, 0, 0)]
    pmax x4, blocking collectives: 1220 us -> 950 us  [by_axis(): return functools.reduce(lax.pmax, axes, x)]
    all_gather x1 -> x0, waiting for transfers between devices: 71.6 us -> none  [per_device(): gathered = lax.all_gather(factors, BLK, axis=0, tiled=True)]
  transfers between devices with their start and end apart: 1 -> 1, of which waited for: 1 -> 0; matrix products, arithmetic and copies ran while one was open for 0% -> 0% of each run, Pallas kernels for 0% -> 0%
where the time goes in v1:
time: 2320 us; the launch traced here: 2300 us
  blocking collectives  950 us (41%)
  starting transfers between devices  840 us (36%)
  other arithmetic  289 us (12%)
  local copies, waits for them, and re-layouts  133 us (6%)
  matrix products  46.1 us (2%)
  loops' own time  29.1 us (1%)
    pmax x4, blocking collectives, by_axis(): return functools.reduce(lax.pmax, axes, x)  950 us
    all_to_all x1, starting transfers between devices, per_device(): lax.all_to_all(jnp.stack([factors] * lax.axis_size(BLK)), BLK, 0, 0)  840 us
    another operation x9, other arithmetic, rotation_of(): left_factor = jnp.linalg.cholesky(identity + 0.25 * outer)  73.2 us
    another operation x6, other arithmetic, rotation_of(): right_factor = jnp.linalg.cholesky(identity + 0.25 * inner)  72.6 us
    another operation x7, other arithmetic, rotation_of(): top_half = jax.scipy.linalg.cho_solve((left_factor, True), top_rows)  63.2 us
    another operation x3, other arithmetic, rotation_of(): low_half = jax.scipy.linalg.cho_solve((right_factor, True), low_rows)  60 us
    another operation x4, local copies, waits for them, and re-layouts, rotate_round(): jnp.stack([matrix[:half_size, :half_size], matrix[half_size:, half_size:]])  51.7 us
  transfers between devices with their start and end apart: 1, of which 0 were waited for; matrix products, arithmetic and copies ran while one was open for 0% of the time, Pallas kernels for 0%

profile of v1, /device:TPU:1, one launch (start us, length us, event | category | flops | bytes accessed | tf_op | source)
XLA Modules:
  0.0 2297.1 jit_solution(4518397182891227333)
XLA Ops:
  9.8 393.3 %conditional.4 = (f32[512,512]{0,1:T(8,128)S(1)}, f32[512,512]{0,1:T(8,128)S(1)}) conditional(s32[]{:T(128)} %convert_element_type.155, (f32[512,512]{1,0:T(8,128)S(1)}, f32[512,512]{0,1:T(8,128)S(1)}) %tuple.70, (f32[512,512]{1,0:T(8,128)S(1)}, f32[512,512]{0,1:T(8,128)S(1)}) %tuple.70), branch_computations={%region_1.2_spmd, %region_2.7_spmd} | conditional | flops 8781105152 | bytes 119010536 | solution.py:128
  10.7 17.2 copy.487
  31.1 23.5 %custom-call.84 = f32[2,128,128]{2,1,0:T(8,128)S(1)} custom-call(f32[2,128,128]{2,1,0:T(8,128)S(1)} %fusion.75), custom_call_target="Cholesky" | custom-call | tf_op jit(solution)/shard_map/cond/branch_1_fun/jit(cholesky)/cholesky | solution.py:55
  55.2 23.5 %custom-call.82 = f32[2,128,128]{2,1,0:T(8,128)S(1)} custom-call(f32[2,128,128]{2,1,0:T(8,128)S(1)} %copy.493), custom_call_target="Cholesky" | custom-call | tf_op jit(solution)/shard_map/cond/branch_1_fun/jit(cholesky)/cholesky | solution.py:54
  79.0 20.1 custom-call.83
  100.0 19.7 custom-call.85
  127.8 3.1 convolution_bitcast_fusion.2
  133.3 17.3 copy.508
  164.2 24.9 %custom-call.88 = f32[2,128,128]{2,1,0:T(8,128)} custom-call(f32[2,128,128]{2,1,0:T(8,128)} %fusion.67), custom_call_target="Cholesky" | custom-call | tf_op jit(solution)/shard_map/cond/branch_1_fun/jit(cholesky)/cholesky | solution.py:55
  189.8 24.3 %custom-call.86 = f32[2,128,128]{2,1,0:T(8,128)S(1)} custom-call(f32[2,128,128]{2,1,0:T(8,128)} %fusion.71), custom_call_target="Cholesky" | custom-call | tf_op jit(solution)/shard_map/cond/branch_1_fun/jit(cholesky)/cholesky | solution.py:54
  217.0 20.7 custom-call.87
  239.4 20.5 custom-call.89
  271.6 3.1 convolution_bitcast_fusion.1
  278.2 17.2 copy.532
  299.2 23.9 %custom-call.92 = f32[2,128,128]{2,1,0:T(8,128)S(1)} custom-call(f32[2,128,128]{2,1,0:T(8,128)S(1)} %fusion.59), custom_call_target="Cholesky" | custom-call | tf_op jit(solution)/shard_map/cond/branch_1_fun/jit(cholesky)/cholesky | solution.py:55
  323.7 23.5 %custom-call.90 = f32[2,128,128]{2,1,0:T(8,128)S(1)} custom-call(f32[2,128,128]{2,1,0:T(8,128)S(1)} %copy.538), custom_call_target="Cholesky" | custom-call | tf_op jit(solution)/shard_map/cond/branch_1_fun/jit(cholesky)/cholesky | solution.py:54
  349.0 19.7 custom-call.91
  369.5 19.8 custom-call.93
  399.5 3.1 convolution_bitcast_fusion
  406.4 12.9 conditional.6
  423.8 11.8 conditional.5
  435.6 8.7 gather_fusion.12
  444.4 9.3 conditional.7
  453.7 9.0 gather_fusion.13
  467.4 11.0 stack.155
  478.4 839.9 %all-to-all-start = ((bf16[32,2,512,512]{3,2,1,0:T(8,128)(2,1)}), bf16[32,2,512,512]{3,2,1,0:T(8,128)(2,1)}, u32[]{:S(2)}, u32[]{:S(2)}) async-start(bf16[32,2,512,512]{3,2,1,0:T(8,128)(2,1)} %stack.155), calls=%async_computation | async-start | bytes 67108864 | tf_op jit(solution)/shard_map/all_to_all | solution.py:147
  1330.2 479.8 %pmax.28 = f32[2]{0:T(128)S(1)} all-reduce(f32[2]{0:T(128)S(1)} %maximum_dynamic-update-slice_fusion), channel_id=1, replica_groups=mesh['blk_0'=4,'blk_1'=4,'blk_2'=2,'grp'=4] {'blk_0'}, use_global_device_ids=true, to_apply=%region_19.22 | all-reduce | flops 2 | bytes 16 | tf_op jit(solution)/shard_map/pmax | solution.py:17
  1810.0 62.5 %pmax.29 = f32[2]{0:T(128)S(1)} all-reduce(f32[2]{0:T(128)S(1)} %pmax.28), channel_id=1, replica_groups=mesh['blk_0'=4,'blk_1'=4,'blk_2'=2,'grp'=4] {'blk_1'}, use_global_device_ids=true, to_apply=%region_20.23 | all-reduce | flops 2 | bytes 16 | tf_op jit(solution)/shard_map/pmax | solution.py:17
  1872.4 5.1 pmax.30
  1877.6 402.1 %pmax.31 = f32[2]{0:T(128)} all-reduce(f32[2]{0:T(128)S(1)} %pmax.30), channel_id=1, replica_groups=mesh['blk_0'=4,'blk_1'=4,'blk_2'=2,'grp'=4] {'grp'}, use_global_device_ids=true, to_apply=%region_22.25 | all-reduce | flops 2 | bytes 16 | tf_op jit(solution)/shard_map/pmax | solution.py:17
  2280.0 6.3 gather_fusion.14
  2286.3 10.6 convert_bitcast_fusion
  (169 shorter events, 97.1 us)
Async XLA Ops:
  78.7 20.5 copy-start.37
  78.9 20.3 copy-start.42
  124.8 139.4 %copy-start.8 = (f32[512,512]{0,1:T(8,128)S(1)}, f32[512,512]{0,1:T(8,128)}, u32[]{:S(2)}) copy-start(f32[512,512]{0,1:T(8,128)} %pad_maximum_fusion.7) | copy-start | bytes 3145732 | tf_op jit(solution)/shard_map/cond
  131.7 0.7 copy-start.23
  259.9 1.7 copy-start.32
  275.6 1.0 copy-start.12
  276.7 0.7 copy-start.22
  423.8 11.9 copy-start
  478.4 845.6 %copy-start.1 = (f32[512,512]{0,1:T(8,128)S(1)}, f32[512,512]{0,1:T(8,128)}, u32[]{:S(2)}) copy-start(f32[512,512]{0,1:T(8,128)} %get-tuple-element.164) | copy-start | bytes 3145732
  478.4 1801.2 %copy-start.47 = (s32[1,32]{1,0:T(1,128)S(1)}, s32[1,32]{1,0:T(1,128)}, u32[]{:S(2)}) copy-start(s32[1,32]{1,0:T(1,128)} %param.26) | copy-start | bytes 388
  478.4 1801.4 %copy-start.48 = (s32[1,64]{1,0:T(1,128)S(1)}, s32[1,64]{1,0:T(1,128)}, u32[]{:S(2)}) copy-start(s32[1,64]{1,0:T(1,128)} %param.27) | copy-start | bytes 772
  478.4 1801.6 %all-to-all-start = ((bf16[32,2,512,512]{3,2,1,0:T(8,128)(2,1)}), bf16[32,2,512,512]{3,2,1,0:T(8,128)(2,1)}, u32[]{:S(2)}, u32[]{:S(2)}) async-start(bf16[32,2,512,512]{3,2,1,0:T(8,128)(2,1)} %stack.155), calls=%async_computation | async-start | bytes 67108864 | tf_op jit(solution)/shard_map/all_to_all | solution.py:147
